TPU v7x, 32 devices: a whole 2x2x4 slice. The times are simulated.
32 devices in a mesh: occ: 8 (over z, core), aux: 4 (over y, x).
Axes of the slice: x: 2, y: 2, z: 4, core: 2. Of those that a mesh axis runs over, the one named last changes fastest.
Arguments:
- integrals: bfloat16 [2048, 256, 512], P('aux', 'occ'), may hold values from -1.1953125 to 1.1953125
- metric: bfloat16 [2048, 2048], replicated, may hold values from -0.125 to 0.125
- e_occ: float32 [256], replicated, may hold values from -2 to -0.3
- e_vir: float32 [512], replicated, may hold values from 0.2 to 3
- partner: int32 [256, 2], P(('occ', 'aux')), may hold values from 0 to 7
- screen: int32 [256, 2], P(('occ', 'aux')), may hold values from 0 to 1
Outputs:
- gradient: bfloat16 [2048, 256, 512], P(None, ('occ', 'aux'))
- density: float32 [512, 512], P('occ')
All inputs are finite; a program needn't handle non-finite values.
Results may differ from a plain program's by a relative error of at most 0.0055.
Values may be sent and summed in bfloat16 or wider, within the bound.
A program may use at most 192 MiB of HBM per device.

v0:
```python
import jax
import jax.numpy as jnp
from jax import lax
from jax.sharding import PartitionSpec as P

NOCC = 256
ROUNDS = 2


def passed_along(array, axis, by):
    count = lax.axis_size(axis)
    return lax.ppermute(array, axis, [(i, (i + by) % count) for i in range(count)])


def transform(metric, moved):
    shape = moved.shape
    mixed = jnp.dot(metric, moved.reshape(shape[0], -1), preferred_element_type=jnp.float32)
    return mixed.astype(jnp.bfloat16).reshape(shape)


def fetch_block(coeff, offset):
    return passed_along(coeff, ("occ", "aux"), offset)


def on_device(integrals, metric, e_occ, e_vir, partner, screen):
    groups = lax.axis_size(("occ", "aux"))
    moved = lax.all_to_all(integrals, "aux", split_axis=1, concat_axis=0, tiled=True)
    coeff = transform(metric, moved)
    naux, own, nvir = coeff.shape
    device = lax.axis_index(("occ", "aux"))
    pair_sum = e_vir[:, None] + e_vir[None, :]
    gamma = jnp.zeros((naux, own, nvir), jnp.float32)
    density = jnp.zeros((nvir, nvir), jnp.float32)
    shifts = (1, groups // 2)
    for rnd in range(ROUNDS):
        offset = shifts[rnd % 2]
        fetched = fetch_block(coeff, offset)
        source = (device - offset) % groups

        def one_pair(carry, slot, rnd=rnd, fetched=fetched, source=source):
            grad_acc, dens_acc = carry
            local = partner[slot, rnd]
            kept = screen[slot, rnd].astype(jnp.float32)
            left = lax.dynamic_index_in_dim(coeff, slot, 1, False)
            right = lax.dynamic_index_in_dim(fetched, local, 1, False)
            intersection = lax.dot_general(
                left, right, (((0,), (0,)), ((), ())), preferred_element_type=jnp.float32
            )
            gap = pair_sum - e_occ[device * own + slot] - e_occ[source * own + local]
            amp = (kept * intersection / gap).astype(jnp.bfloat16)
            term = lax.dot_general(
                right, amp, (((1,), (1,)), ((), ())), preferred_element_type=jnp.float32
            )
            column = lax.dynamic_index_in_dim(grad_acc, slot, 1, False) + term
            grad_acc = lax.dynamic_update_index_in_dim(grad_acc, column, slot, 1)
            dens_acc = dens_acc + lax.dot_general(
                amp, amp, (((1,), (1,)), ((), ())), preferred_element_type=jnp.float32
            )
            return (grad_acc, dens_acc)

        def visit(slot, carry, rnd=rnd, one_pair=one_pair):
            return one_pair(carry, slot)

        gamma, density = lax.fori_loop(0, own, visit, (gamma, density))
    total = lax.psum(density, ("occ", "aux"))
    height = nvir // lax.axis_size("occ")
    block = lax.dynamic_slice_in_dim(total, lax.axis_index("occ") * height, height, 0)
    return (gamma.astype(jnp.bfloat16), block / NOCC)


def solution(mesh):
    placed = (
        P("aux", "occ", None),
        P(),
        P(),
        P(),
        P(("occ", "aux"), None),
        P(("occ", "aux"), None),
    )
    return jax.shard_map(
        on_device,
        mesh=mesh,
        in_specs=placed,
        out_specs=(P(None, ("occ", "aux"), None), P("occ", None)),
        check_vma=False,
    )
```

profile of v0, /device:TPU:0, one launch (start us, length us, event | category | flops | bytes accessed | tf_op | source)
XLA Modules:
  0.0 1485.5 jit_solution(9783774959772987957)
XLA Ops:
  7.2 12.0 copy.15
  19.3 187.7 %all_to_all.15 = bf16[512,32,512]{2,0,1:T(8,128)(2,1)S(1)} all-to-all(bf16[512,32,512]{2,0,1:T(8,128)(2,1)S(1)} %copy.15), channel_id=1, replica_groups=mesh['occ'=8,'aux'=4] {'aux'}, dimensions={1} | all-to-all | bytes 33554432 | tf_op jit(solution)/shard_map/all_to_all | solution.py:27
  206.9 38.4 %copy.16 = bf16[512,4,8,512]{3,2,0,1:T(8,128)(2,1)S(1)} copy(bf16[512,4,8,512]{3,0,2,1:T(8,128)(2,1)S(1)} %bitcast.109) | data formatting | bytes 33554432 | tf_op jit(solution)/shard_map/all_to_all | solution.py:27
  245.4 10.5 copy.23
  255.9 38.5 %convolution_convert_fusion = bf16[2048,4096]{1,0:T(8,128)(2,1)S(1)} fusion(bf16[2048,2048]{1,0:T(8,128)(2,1)S(1)} %bitcast.114, bf16[2048,4096]{1,0:T(8,128)(2,1)} %bitcast.111), kind=kOutput, calls=%fused_computation.42 | convolution fusion | flops 34368126976 | bytes 41943040 | tf_op jit(solution)/shard_map/dot_general | solution.py:17
  294.4 7.4 copy.27
  302.8 2.6 collective-permute-start.1
  305.4 362.3 %collective-permute-done = bf16[2048,8,512]{2,0,1:T(8,128)(2,1)} collective-permute-done((bf16[2048,8,512]{2,0,1:T(8,128)(2,1)}, bf16[2048,8,512]{2,0,1:T(8,128)(2,1)}, u32[]{:S(2)}, u32[]{:S(2)}) %collective-permute-start) | collective-permute-done | bytes 16777248 | tf_op jit(solution)/shard_map/ppermute | solution.py:12
  667.7 11.3 broadcast_in_dim.27
  679.0 138.9 %while.37 = (s32[]{:T(128)}, f32[2048,8,512]{2,0,1:T(8,128)}, f32[512,512]{1,0:T(8,128)S(1)}, s32[8,2]{0,1:T(2,128)S(1)}, bf16[2048,8,512]{2,0,1:T(8,128)(2,1)},...) while((s32[]{:T(128)}, f32[2048,8,512]{2,0,1:T(8,128)}, ...), condition=%wide.region_1.2_spmd.clone, body=%wide.region_0.1_spmd.clone.sunk | while | flops 2419064832 | bytes 26745676 | solution.py:64
  682.8 5.4 fusion.79
  688.2 2.6 constant_dynamic-slice_fusion.12
  690.8 4.9 bitcast_dynamic-update-slice_fusion.5
  700.1 5.4 fusion.79
  705.5 2.6 constant_dynamic-slice_fusion.12
  708.2 4.9 bitcast_dynamic-update-slice_fusion.5
  717.5 5.4 fusion.79
  722.9 2.6 constant_dynamic-slice_fusion.12
  725.6 4.9 bitcast_dynamic-update-slice_fusion.5
  734.9 5.4 fusion.79
  740.3 2.6 constant_dynamic-slice_fusion.12
  742.9 4.9 bitcast_dynamic-update-slice_fusion.5
  752.2 5.4 fusion.79
  757.6 2.6 constant_dynamic-slice_fusion.12
  760.3 4.9 bitcast_dynamic-update-slice_fusion.5
  769.6 5.4 fusion.79
  775.0 2.6 constant_dynamic-slice_fusion.12
  777.6 4.9 bitcast_dynamic-update-slice_fusion.5
  787.0 5.4 fusion.79
  792.4 2.6 constant_dynamic-slice_fusion.12
  795.0 4.9 bitcast_dynamic-update-slice_fusion.5
  804.3 5.4 fusion.79
  809.7 2.6 constant_dynamic-slice_fusion.12
  812.4 4.9 bitcast_dynamic-update-slice_fusion.5
  817.9 206.2 %collective-permute-done.1 = bf16[2048,8,512]{2,0,1:T(8,128)(2,1)} collective-permute-done((bf16[2048,8,512]{2,0,1:T(8,128)(2,1)}, bf16[2048,8,512]{2,0,1:T(8,128)(2,1)}, u32[]{:S(2)}, u32[]{:S(2)}) %collective-permute-start.1) | collective-permute-done | bytes 16777248 | tf_op jit(solution)/shard_map/ppermute | solution.py:12
  1024.1 140.7 %while.36 = (s32[]{:T(128)}, f32[2048,8,512]{2,0,1:T(8,128)}, f32[512,512]{1,0:T(8,128)S(1)}, s32[8,2]{0,1:T(2,128)S(1)}, bf16[2048,8,512]{2,0,1:T(8,128)(2,1)},...) while((s32[]{:T(128)}, f32[2048,8,512]{2,0,1:T(8,128)}, ...), condition=%wide.region_3.4_spmd.clone, body=%wide.region_2.3_spmd.clone.sunk | while | flops 2418802688 | bytes 26745668 | solution.py:64
  1028.2 5.4 fusion.71
  1033.6 2.6 constant_dynamic-slice_fusion.10
  1036.3 4.9 bitcast_dynamic-update-slice_fusion.4
  1045.8 5.4 fusion.71
  1051.2 2.6 constant_dynamic-slice_fusion.10
  1053.9 4.9 bitcast_dynamic-update-slice_fusion.4
  1063.4 5.4 fusion.71
  1068.8 2.6 constant_dynamic-slice_fusion.10
  1071.5 4.9 bitcast_dynamic-update-slice_fusion.4
  1081.0 5.4 fusion.71
  1086.4 2.6 constant_dynamic-slice_fusion.10
  1089.1 4.9 bitcast_dynamic-update-slice_fusion.4
  1098.6 5.4 fusion.71
  1104.0 2.6 constant_dynamic-slice_fusion.10
  1106.6 4.9 bitcast_dynamic-update-slice_fusion.4
  1116.2 5.4 fusion.71
  1121.6 2.6 constant_dynamic-slice_fusion.10
  1124.2 4.9 bitcast_dynamic-update-slice_fusion.4
  1133.8 5.4 fusion.71
  1139.2 2.6 constant_dynamic-slice_fusion.10
  1141.8 4.9 bitcast_dynamic-update-slice_fusion.4
  1151.4 5.4 fusion.71
  1156.8 2.6 constant_dynamic-slice_fusion.10
  1159.4 4.9 bitcast_dynamic-update-slice_fusion.4
  1164.8 1.0 copy-done
  1165.8 31.3 %copy.26 = bf16[2048,8,512]{2,1,0:T(8,128)(2,1)} copy(f32[2048,8,512]{2,0,1:T(8,128)} %get-tuple-element.518) | data formatting | bytes 50331648 | tf_op jit(solution)/shard_map/while | solution.py:64
  1197.1 280.0 %all-reduce.2.cloned.1.call-done = f32[512,512]{1,0:T(8,128)} async-done(((f32[512,512]{1,0:T(8,128)}), f32[512,512]{1,0:T(8,128)}) %all-reduce.2.cloned.1.call-update) | async-done | bytes 1048592 | tf_op jit(solution)/shard_map/psum | solution.py:65
  1477.1 1.6 dynamic-slice_multiply_fusion
  (66 shorter events, 30.9 us)
Async XLA Ops:
  7.2 1469.9 %all-reduce.2.cloned.1.call-start = ((), (), s32[]{:S(2)}) async-start(), calls=%async_computation.1 | async-start | bytes 2097152 | tf_op jit(solution)/shard_map/psum | solution.py:65
  206.9 49.0 %slice-start = ((s8[8388608]{0:T(1024)(128)(4,1)}), s8[4194304]{0:T(1024)(128)(4,1)S(1)}, s32[]{:S(2)}) async-start(s8[8388608]{0:T(1024)(128)(4,1)} %bitcast.113), calls=%async_computation.2 | async-start | bytes 8388608
  245.3 10.5 slice-start.1
  301.9 365.8 %collective-permute-start = (bf16[2048,8,512]{2,0,1:T(8,128)(2,1)}, bf16[2048,8,512]{2,0,1:T(8,128)(2,1)}, u32[]{:S(2)}, u32[]{:S(2)}) collective-permute-start(bf16[2048,8,512]{2,0,1:T(8,128)(2,1)} %bitcast.60), channel_id=1, source_target_pairs={{0,1},{1,2},{2,3},{3,4},{4,5},{5,6},{6,7},{7,8},{8,9},{9,10},{10,1... | collective-permute-start | bytes 50331656 | tf_op jit(solution)/shard_map/ppermute | solution.py:12
  302.8 721.3 %collective-permute-start.1 = (bf16[2048,8,512]{2,0,1:T(8,128)(2,1)}, bf16[2048,8,512]{2,0,1:T(8,128)(2,1)}, u32[]{:S(2)}, u32[]{:S(2)}) collective-permute-start(bf16[2048,8,512]{2,0,1:T(8,128)(2,1)} %bitcast.60), channel_id=1, source_target_pairs={{0,16},{1,17},{2,18},{3,19},{4,20},{5,21},{6,22},{7,23},{8,24},{9,... | collective-permute-start | bytes 50331656 | tf_op jit(solution)/shard_map/ppermute | solution.py:12
  305.4 373.5 %copy-start.1 = (f32[256]{0:T(256)S(1)}, f32[256]{0:T(256)}, u32[]{:S(2)}) copy-start(f32[256]{0:T(256)} %param.12) | copy-start | bytes 3076
  305.4 373.6 %copy-start.2 = (s32[8,2]{0,1:T(2,128)S(1)}, s32[8,2]{0,1:T(2,128)}, u32[]{:S(2)}) copy-start(s32[8,2]{0,1:T(2,128)} %param.14) | copy-start | bytes 196
  305.4 373.6 %copy-start.3 = (s32[8,2]{0,1:T(2,128)S(1)}, s32[8,2]{0,1:T(2,128)}, u32[]{:S(2)}) copy-start(s32[8,2]{0,1:T(2,128)} %param.15) | copy-start | bytes 196
  305.4 373.6 %copy-start.4 = (f32[512]{0:T(512)S(1)}, f32[512]{0:T(512)}, u32[]{:S(2)}) copy-start(f32[512]{0:T(512)} %param.13) | copy-start | bytes 6148
  1164.8 1.0 copy-start
Sparse Core Ops, SparseCore 0:
  1165.9 311.0 all-reduce.1
where the time goes:
time: 1490 us
  waiting for transfers between devices  848 us (57%)
  matrix products  212 us (14%)
  blocking collectives  188 us (13%)
  local copies, waits for them, and re-layouts  165 us (11%)
  loops' own time  42.8 us (3%)
    ppermute x2, waiting for transfers between devices, passed_along(): lax.ppermute(array, axis, [(i, (i + by) % count) for i in range(count)])  568 us
    psum x1, waiting for transfers between devices, on_device(): total = lax.psum(density, ('occ', 'aux'))  280 us
    all_to_all x1, blocking collectives, on_device(): lax.all_to_all(integrals, 'aux', split_axis=1, concat_axis=0, tiled=True)  188 us
    dot_general x16, matrix products, one_pair(): lax.dot_general(left, right, (((0,), (0,)), ((), ())), preferred_element_...  86.2 us
    dot_general x16, matrix products, one_pair(): lax.dot_general(right, amp, (((1,), (1,)), ((), ())), preferred_element_t...  78.6 us
    another operation x2, loops' own time, on_device(): gamma, density = lax.fori_loop(0, own, visit, (gamma, density))  42.8 us
    dynamic_slice x16, local copies, waits for them, and re-layouts, one_pair(): column = lax.dynamic_index_in_dim(grad_acc, slot, 1, False) + term  42.2 us
    dot_general x1, matrix products, transform(): jnp.dot(metric, moved.reshape(shape[0], -1), preferred_element_type=jnp.f...  38.5 us
  transfers between devices with their start and end apart: 3, of which 3 were waited for; matrix products, arithmetic and copies ran while one was open for 11% of the time, Pallas kernels for 0%

commit v1 on v0

--- a/solution.py
+++ b/solution.py
@@ -23,6 +23,11 @@
 
 
 def on_device(integrals, metric, e_occ, e_vir, partner, screen):
+
+    def _detail_sectors(in_array):
+        current_arr = lax.all_gather(in_array, ("occ", "aux")).sum(axis=0)
+        return current_arr
+
     groups = lax.axis_size(("occ", "aux"))
     moved = lax.all_to_all(integrals, "aux", split_axis=1, concat_axis=0, tiled=True)
     coeff = transform(metric, moved)
@@ -62,7 +67,7 @@
             return one_pair(carry, slot)
 
         gamma, density = lax.fori_loop(0, own, visit, (gamma, density))
-    total = lax.psum(density, ("occ", "aux"))
+    total = _detail_sectors(density)
     height = nvir // lax.axis_size("occ")
     block = lax.dynamic_slice_in_dim(total, lax.axis_index("occ") * height, height, 0)
     return (gamma.astype(jnp.bfloat16), block / NOCC)

time: 1490 us -> 1560 us (1.047)
  waiting for transfers between devices: 848 us -> 913 us
    all_gather x0 -> x1, waiting for transfers between devices: none -> 343 us  [_detail_sectors(): current_arr = lax.all_gather(in_array, ('occ', 'aux')).sum(axis=0)]
    psum x1 -> x0, waiting for transfers between devices: 280 us -> none  [on_device(): total = lax.psum(density, ('occ', 'aux'))]
  transfers between devices with their start and end apart: 3 -> 3, of which waited for: 3 -> 3; matrix products, arithmetic and copies ran while one was open for 11% -> 10% of each run, Pallas kernels for 0% -> 0%
where the time goes in v1:
time: 1560 us
  waiting for transfers between devices  913 us (59%)
  matrix products  211 us (14%)
  blocking collectives  188 us (12%)
  local copies, waits for them, and re-layouts  165 us (11%)
  loops' own time  42.8 us (3%)
  other arithmetic  23.5 us (2%)
    ppermute x2, waiting for transfers between devices, passed_along(): lax.ppermute(array, axis, [(i, (i + by) % count) for i in range(count)])  569 us
    all_gather x1, waiting for transfers between devices, _detail_sectors(): current_arr = lax.all_gather(in_array, ('occ', 'aux')).sum(axis=0)  343 us
    all_to_all x1, blocking collectives, on_device(): lax.all_to_all(integrals, 'aux', split_axis=1, concat_axis=0, tiled=True)  188 us
    dot_general x16, matrix products, one_pair(): lax.dot_general(left, right, (((0,), (0,)), ((), ())), preferred_element_...  86.2 us
    dot_general x16, matrix products, one_pair(): lax.dot_general(right, amp, (((1,), (1,)), ((), ())), preferred_element_t...  77.5 us
    another operation x2, loops' own time, on_device(): gamma, density = lax.fori_loop(0, own, visit, (gamma, density))  42.8 us
    dynamic_slice x16, local copies, waits for them, and re-layouts, one_pair(): column = lax.dynamic_index_in_dim(grad_acc, slot, 1, False) + term  42.2 us
    dot_general x1, matrix products, transform(): jnp.dot(metric, moved.reshape(shape[0], -1), preferred_element_type=jnp.f...  38.5 us
  transfers between devices with their start and end apart: 3, of which 3 were waited for; matrix products, arithmetic and copies ran while one was open for 10% of the time, Pallas kernels for 0%

profile of v1, /device:TPU:0, one launch (start us, length us, event | category | flops | bytes accessed | tf_op | source)
XLA Modules:
  0.0 1559.7 jit_solution(4194682730207056767)
XLA Ops:
  7.2 12.0 copy.15
  19.3 187.7 %all_to_all.15 = bf16[512,32,512]{2,0,1:T(8,128)(2,1)S(1)} all-to-all(bf16[512,32,512]{2,0,1:T(8,128)(2,1)S(1)} %copy.15), channel_id=1, replica_groups=mesh['occ'=8,'aux'=4] {'aux'}, dimensions={1} | all-to-all | bytes 33554432 | tf_op jit(solution)/shard_map/all_to_all | solution.py:32
  206.9 38.4 %copy.16 = bf16[512,4,8,512]{3,2,0,1:T(8,128)(2,1)S(1)} copy(bf16[512,4,8,512]{3,0,2,1:T(8,128)(2,1)S(1)} %bitcast.110) | data formatting | bytes 33554432 | tf_op jit(solution)/shard_map/all_to_all | solution.py:32
  245.4 10.5 copy.23
  255.8 38.5 %convolution_convert_fusion = bf16[2048,4096]{1,0:T(8,128)(2,1)S(1)} fusion(bf16[2048,2048]{1,0:T(8,128)(2,1)S(1)} %bitcast.116, bf16[2048,4096]{1,0:T(8,128)(2,1)} %bitcast.113), kind=kOutput, calls=%fused_computation.42 | convolution fusion | flops 34368126976 | bytes 41943040 | tf_op jit(solution)/shard_map/dot_general | solution.py:17
  294.3 7.4 copy.27
  302.7 2.6 collective-permute-start.1
  305.3 362.3 %collective-permute-done = bf16[2048,8,512]{2,0,1:T(8,128)(2,1)} collective-permute-done((bf16[2048,8,512]{2,0,1:T(8,128)(2,1)}, bf16[2048,8,512]{2,0,1:T(8,128)(2,1)}, u32[]{:S(2)}, u32[]{:S(2)}) %collective-permute-start) | collective-permute-done | bytes 16777248 | tf_op jit(solution)/shard_map/ppermute | solution.py:12
  667.5 11.3 broadcast_in_dim.27
  678.8 138.3 %while.37 = (s32[]{:T(128)}, f32[2048,8,512]{2,0,1:T(8,128)}, f32[512,512]{1,0:T(8,128)S(1)}, s32[8,2]{0,1:T(2,128)S(1)}, bf16[2048,8,512]{2,0,1:T(8,128)(2,1)},...) while((s32[]{:T(128)}, f32[2048,8,512]{2,0,1:T(8,128)}, ...), condition=%wide.region_1.2_spmd.clone, body=%wide.region_0.1_spmd.clone.sunk | while | flops 2419064832 | bytes 26745676 | solution.py:69
  682.6 5.4 fusion.79
  688.0 2.6 constant_dynamic-slice_fusion.12
  690.7 4.8 bitcast_dynamic-update-slice_fusion.5
  699.9 5.4 fusion.79
  705.3 2.6 constant_dynamic-slice_fusion.12
  708.0 4.9 bitcast_dynamic-update-slice_fusion.5
  717.2 5.4 fusion.79
  722.6 2.6 constant_dynamic-slice_fusion.12
  725.3 4.9 bitcast_dynamic-update-slice_fusion.5
  734.5 5.4 fusion.79
  739.9 2.6 constant_dynamic-slice_fusion.12
  742.6 4.8 bitcast_dynamic-update-slice_fusion.5
  751.8 5.4 fusion.79
  757.2 2.6 constant_dynamic-slice_fusion.12
  759.8 4.8 bitcast_dynamic-update-slice_fusion.5
  769.1 5.4 fusion.79
  774.5 2.6 constant_dynamic-slice_fusion.12
  777.1 4.9 bitcast_dynamic-update-slice_fusion.5
  786.4 5.4 fusion.79
  791.8 2.6 constant_dynamic-slice_fusion.12
  794.4 4.9 bitcast_dynamic-update-slice_fusion.5
  803.7 5.4 fusion.79
  809.1 2.6 constant_dynamic-slice_fusion.12
  811.7 4.8 bitcast_dynamic-update-slice_fusion.5
  817.2 206.8 %collective-permute-done.1 = bf16[2048,8,512]{2,0,1:T(8,128)(2,1)} collective-permute-done((bf16[2048,8,512]{2,0,1:T(8,128)(2,1)}, bf16[2048,8,512]{2,0,1:T(8,128)(2,1)}, u32[]{:S(2)}, u32[]{:S(2)}) %collective-permute-start.1) | collective-permute-done | bytes 16777248 | tf_op jit(solution)/shard_map/ppermute | solution.py:12
  1024.0 140.2 %while.36 = (s32[]{:T(128)}, f32[2048,8,512]{2,0,1:T(8,128)}, f32[512,512]{1,0:T(8,128)S(1)}, s32[8,2]{0,1:T(2,128)S(1)}, bf16[2048,8,512]{2,0,1:T(8,128)(2,1)},...) while((s32[]{:T(128)}, f32[2048,8,512]{2,0,1:T(8,128)}, ...), condition=%wide.region_3.4_spmd.clone, body=%wide.region_2.3_spmd.clone.sunk | while | flops 2418802688 | bytes 26745668 | solution.py:69
  1028.1 5.4 fusion.71
  1033.5 2.6 constant_dynamic-slice_fusion.10
  1036.1 4.8 bitcast_dynamic-update-slice_fusion.4
  1045.6 5.4 fusion.71
  1051.0 2.6 constant_dynamic-slice_fusion.10
  1053.7 4.9 bitcast_dynamic-update-slice_fusion.4
  1063.2 5.4 fusion.71
  1068.6 2.6 constant_dynamic-slice_fusion.10
  1071.2 4.9 bitcast_dynamic-update-slice_fusion.4
  1080.7 5.4 fusion.71
  1086.1 2.6 constant_dynamic-slice_fusion.10
  1088.7 4.8 bitcast_dynamic-update-slice_fusion.4
  1098.2 5.4 fusion.71
  1103.6 2.6 constant_dynamic-slice_fusion.10
  1106.2 4.8 bitcast_dynamic-update-slice_fusion.4
  1115.7 5.4 fusion.71
  1121.1 2.6 constant_dynamic-slice_fusion.10
  1123.7 4.9 bitcast_dynamic-update-slice_fusion.4
  1133.2 5.4 fusion.71
  1138.6 2.6 constant_dynamic-slice_fusion.10
  1141.3 4.9 bitcast_dynamic-update-slice_fusion.4
  1150.8 5.4 fusion.71
  1156.2 2.6 constant_dynamic-slice_fusion.10
  1158.8 4.8 bitcast_dynamic-update-slice_fusion.4
  1164.1 1.0 copy-done
  1165.1 31.3 %copy.26 = bf16[2048,8,512]{2,1,0:T(8,128)(2,1)} copy(f32[2048,8,512]{2,0,1:T(8,128)} %get-tuple-element.518) | data formatting | bytes 50331648 | tf_op jit(solution)/shard_map/while | solution.py:69
  1196.4 343.5 %all-gather.3.cloned.1.call-done = f32[16384,512]{1,0:T(8,128)} async-done(((f32[512,512]{1,0:T(8,128)}), f32[16384,512]{1,0:T(8,128)}) %all-gather.3.cloned.1.call-update) | async-done | bytes 33554448 | tf_op jit(solution)/shard_map/all_gather | solution.py:28
  1539.9 12.3 reduce_sum.9
  (67 shorter events, 31.5 us)
Async XLA Ops:
  7.2 1532.7 %all-gather.3.cloned.1.call-start = ((), (), s32[]{:S(2)}) async-start(), calls=%async_computation.1 | async-start | bytes 34603008 | tf_op jit(solution)/shard_map/all_gather | solution.py:28
  206.9 48.9 %slice-start = ((s8[8388608]{0:T(1024)(128)(4,1)}), s8[4194304]{0:T(1024)(128)(4,1)S(1)}, s32[]{:S(2)}) async-start(s8[8388608]{0:T(1024)(128)(4,1)} %bitcast.115), calls=%async_computation.2 | async-start | bytes 8388608
  245.3 10.5 slice-start.1
  301.7 365.8 %collective-permute-start = (bf16[2048,8,512]{2,0,1:T(8,128)(2,1)}, bf16[2048,8,512]{2,0,1:T(8,128)(2,1)}, u32[]{:S(2)}, u32[]{:S(2)}) collective-permute-start(bf16[2048,8,512]{2,0,1:T(8,128)(2,1)} %bitcast.61), channel_id=1, source_target_pairs={{0,1},{1,2},{2,3},{3,4},{4,5},{5,6},{6,7},{7,8},{8,9},{9,10},{10,1... | collective-permute-start | bytes 50331656 | tf_op jit(solution)/shard_map/ppermute | solution.py:12
  302.7 721.3 %collective-permute-start.1 = (bf16[2048,8,512]{2,0,1:T(8,128)(2,1)}, bf16[2048,8,512]{2,0,1:T(8,128)(2,1)}, u32[]{:S(2)}, u32[]{:S(2)}) collective-permute-start(bf16[2048,8,512]{2,0,1:T(8,128)(2,1)} %bitcast.61), channel_id=1, source_target_pairs={{0,16},{1,17},{2,18},{3,19},{4,20},{5,21},{6,22},{7,23},{8,24},{9,... | collective-permute-start | bytes 50331656 | tf_op jit(solution)/shard_map/ppermute | solution.py:12
  305.2 373.5 %copy-start.1 = (f32[256]{0:T(256)S(1)}, f32[256]{0:T(256)}, u32[]{:S(2)}) copy-start(f32[256]{0:T(256)} %param.12) | copy-start | bytes 3076
  305.2 373.6 %copy-start.2 = (s32[8,2]{0,1:T(2,128)S(1)}, s32[8,2]{0,1:T(2,128)}, u32[]{:S(2)}) copy-start(s32[8,2]{0,1:T(2,128)} %param.14) | copy-start | bytes 196
  305.2 373.6 %copy-start.3 = (s32[8,2]{0,1:T(2,128)S(1)}, s32[8,2]{0,1:T(2,128)}, u32[]{:S(2)}) copy-start(s32[8,2]{0,1:T(2,128)} %param.15) | copy-start | bytes 196
  305.2 373.6 %copy-start.4 = (f32[512]{0:T(512)S(1)}, f32[512]{0:T(512)}, u32[]{:S(2)}) copy-start(f32[512]{0:T(512)} %param.13) | copy-start | bytes 6148
  1164.1 1.0 copy-start
Sparse Core Ops, SparseCore 0:
  1165.3 374.5 all-gather.2
